TPU v7x, 32 devices: a whole 2x2x4 slice. The times are simulated.
32 devices in a mesh: head: 8 (over z, x), client: 4 (over y, core).
Axes of the slice: x: 2, y: 2, z: 4, core: 2. Of those that a mesh axis runs over, the one named last changes fastest.
Arguments:
- client_ids: int32 [32], replicated, may hold values from 0 to 127, as said below
- client_table: bfloat16 [128, 256], replicated, may hold values from -6 to 6
- in_weight: bfloat16 [256, 4096], P(None, 'client'), may hold values from -0.375 to 0.375
- in_bias: float32 [4096], P('client'), may hold values from -3 to 3
- head_weight: bfloat16 [4096, 131072], P('client', 'head'), may hold values from -0.09375 to 0.09375
- tokens: int32 [32, 256], P(('head', 'client')), may hold values from 0 to 255
- labels: int32 [32, 256], P(('head', 'client')), may hold values from 0 to 255
- byte_table: bfloat16 [256, 4096], P(None, 'client'), may hold values from -5.5 to 6.7
- out_table: bfloat16 [256, 4096], P(None, 'client'), may hold values from -5.625 to 5.625
Outputs:
- head_grad: bfloat16 [4096, 131072], P('client', 'head')
- in_grad: float32 [256, 4096], P(None, 'client')
- losses: float32 [32], P(('head', 'client'))
Inputs may be any that keep to these rules, and one draw needn't show every extreme that they name: `client_ids`: distinct population indices.
All inputs are finite; a program needn't handle non-finite values.
Results may differ from a plain program's by a relative error of at most 0.0085.
Values may be sent and summed in bfloat16 or wider, within the bound.
A program may use at most 128 MiB of HBM per device.

v0:
```python
import jax
import jax.numpy as jnp
from jax import lax
from jax.sharding import PartitionSpec as P

EPSILON = 1e-06
learn_rate = 0.1


def client_loss(factor_a, factor_b, inputs, label_row, out_table):
    depth = factor_a.shape[0]
    rank_size = factor_a.shape[1]
    normed_in = inputs * lax.rsqrt(jnp.mean(inputs * inputs, -1, keepdims=True) + EPSILON)
    low_rank = jnp.dot(normed_in, factor_a, precision=lax.Precision.HIGHEST)
    adapted = inputs + jnp.dot(low_rank, factor_b, precision=lax.Precision.HIGHEST) / jnp.sqrt(
        jnp.float32(depth * rank_size)
    )
    normed = (adapted * lax.rsqrt(jnp.mean(adapted * adapted, -1, keepdims=True) + EPSILON)).astype(
        jnp.bfloat16
    )
    logits = lax.dot_general(
        normed, out_table, (((1,), (1,)), ((), ())), preferred_element_type=jnp.float32
    )
    logits = logits * (4.0 / jnp.sqrt(jnp.float32(depth)))
    log_total = jax.nn.logsumexp(logits, -1)
    vocab_ids = lax.broadcasted_iota(jnp.int32, logits.shape, 1)
    picked = jnp.sum(jnp.where(vocab_ids == label_row[:, None], logits, 0.0), -1)
    return jnp.sum(log_total - picked)


def train_client(factor_row, token_row, label_row, byte_table, out_table):
    depth = byte_table.shape[1]
    split_at = factor_row.shape[0] // 2
    rank_size = split_at // depth
    start_a = factor_row[:split_at].reshape(depth, rank_size).astype(jnp.float32)
    start_b = factor_row[split_at:].reshape(rank_size, depth).astype(jnp.float32)
    onehot = (
        token_row[:, None]
        == lax.broadcasted_iota(jnp.int32, (token_row.shape[0], byte_table.shape[0]), 1)
    ).astype(jnp.bfloat16)
    inputs = jnp.dot(onehot, byte_table, preferred_element_type=jnp.float32)
    loss_grad = jax.value_and_grad(client_loss, argnums=(0, 1))
    first_loss, (grad_a, grad_b) = loss_grad(start_a, start_b, inputs, label_row, out_table)
    middle_a = start_a - learn_rate * grad_a
    middle_b = start_b - learn_rate * grad_b
    second_loss, (grad_a, grad_b) = loss_grad(middle_a, middle_b, inputs, label_row, out_table)
    final_a = middle_a - learn_rate * grad_a
    final_b = middle_b - learn_rate * grad_b
    deltas = jnp.concatenate(
        [(final_a - start_a).reshape(-1), (final_b - start_b).reshape(-1)]
    ).astype(jnp.bfloat16)
    return (deltas, first_loss / token_row.shape[0])


def local(
    client_ids, client_table, in_weight, in_bias, head_weight, tokens, labels, byte_table, out_table
):
    head_count = lax.axis_size("head")
    group_count = lax.axis_size("client")
    per_device = tokens.shape[0]
    byte_full, out_full = (
        lax.all_gather(byte_table, "client", axis=1, tiled=True),
        lax.all_gather(out_table, "client", axis=1, tiled=True),
    )
    ordered = client_ids.reshape(head_count, group_count, per_device).transpose(1, 0, 2).reshape(-1)
    chosen = client_table[ordered]
    preact = jnp.dot(chosen, in_weight, preferred_element_type=jnp.float32) + in_bias
    hidden = jnp.maximum(preact, 0.0).astype(jnp.bfloat16)
    hidden_rows = hidden
    summed = lax.psum_scatter(
        jnp.dot(hidden_rows, head_weight, preferred_element_type=jnp.float32),
        "client",
        scatter_dimension=0,
        tiled=True,
    )
    owned = lax.all_to_all(
        summed.astype(jnp.bfloat16), "head", split_axis=0, concat_axis=1, tiled=True
    )

    def run_client(record):
        return train_client(record[0], record[1], record[2], byte_full, out_full)

    deltas, losses = lax.map(run_client, (owned, tokens, labels))
    returned = lax.all_to_all(deltas, "head", split_axis=1, concat_axis=0, tiled=True)
    received = lax.all_gather(returned, "client", axis=0, tiled=True)
    hidden_rows = hidden
    grad_sum = lax.dot_general(
        hidden_rows, received, (((0,), (0,)), ((), ())), preferred_element_type=jnp.float32
    )
    partial_value = lax.dot_general(
        received, head_weight, (((1,), (1,)), ((), ())), preferred_element_type=jnp.float32
    )
    hidden_back = partial_value
    grad_sum, hidden_back = (grad_sum, hidden_back)
    hidden_back = lax.psum(hidden_back, "head")
    masked = jnp.where(preact > 0, hidden_back, 0.0)
    in_grad = lax.dot_general(
        chosen.astype(jnp.float32),
        masked,
        (((0,), (0,)), ((), ())),
        precision=lax.Precision.HIGHEST,
    )
    return (grad_sum.astype(jnp.bfloat16), in_grad, losses)


def solution(mesh):
    placed = (
        P(),
        P(),
        P(None, "client"),
        P("client"),
        P("client", "head"),
        P(("head", "client"), None),
        P(("head", "client"), None),
        P(None, "client"),
        P(None, "client"),
    )
    return jax.shard_map(
        local,
        mesh=mesh,
        in_specs=placed,
        out_specs=(P("client", "head"), P(None, "client"), P(("head", "client"))),
        check_vma=False,
    )
```

profile of v0, /device:TPU:0, one launch (start us, length us, event | category | flops | bytes accessed | tf_op | source)
XLA Modules:
  0.0 274.1 jit_solution(7337150185194927193)
XLA Ops:
  7.2 0.0 reduce-scatter.2.cloned.1.call-start
  7.2 0.8 reshape.166
  8.0 0.1 copy.22
  8.1 0.1 reshape.167
  8.2 1.5 gather_fusion
  9.7 0.9 convolution_add_fusion
  10.5 14.9 %fusion.59 = f32[32,16384]{1,0:T(8,128)} fusion(bf16[1024,16384]{1,0:T(8,128)(2,1)} %param.13, f32[32,1024]{1,0:T(8,128)S(1)} %convolution_add_fusion), kind=kOutput, calls=%fused_computation.91 | convolution fusion | flops 1073807360 | bytes 35782656 | tf_op jit(solution)/shard_map/dot_general | solution.py:71
  25.4 0.0 reduce-scatter.2.cloned.1.call-update
  25.4 0.0 all-gather.5.cloned.1.call-start
  25.5 0.7 all-gather.5.cloned.1.call-update
  26.2 0.0 all-gather.7.cloned.1.call-start
  26.2 0.7 all-gather.7.cloned.1.call-update
  26.9 32.6 %reduce-scatter.2.cloned.1.call-done = f32[8,16384]{1,0:T(8,128)} async-done(((f32[32,16384]{1,0:T(8,128)}), f32[8,16384]{1,0:T(8,128)}) %reduce-scatter.2.cloned.1.call-update) | async-done | bytes 524304 | tf_op jit(solution)/shard_map/reduce_scatter | solution.py:70
  59.5 1.1 convert_bitcast_fusion
  60.6 0.5 broadcast.217
  61.1 0.8 reduce.4
  61.9 0.9 reshape.181
  62.8 5.5 %all-to-all-start = ((bf16[8,2,8192]{2,1,0:T(2,128)(2,1)}), bf16[8,2,8192]{2,1,0:T(2,128)(2,1)S(1)}, u32[]{:S(2)}, u32[]{:S(2)}) async-start(bf16[8,2,8192]{2,1,0:T(2,128)(2,1)} %reshape.181), calls=%async_computation.1 | async-start | bytes 524288 | tf_op jit(solution)/shard_map/all_to_all | solution.py:76
  68.3 0.0 all-gather.9.cloned.1.call-start
  68.3 15.3 %all-gather.5.cloned.1.call-done = bf16[256,4096]{1,0:T(8,128)(2,1)} async-done(((bf16[256,1024]{1,0:T(8,128)(2,1)}), bf16[256,4096]{1,0:T(8,128)(2,1)}) %all-gather.5.cloned.1.call-update) | async-done | bytes 2097168 | tf_op jit(solution)/shard_map/all_gather | solution.py:62
  83.7 4.4 %multiply_reduce_fusion.2 = (f32[256]{0:T(256)S(1)}, f32[256,4096]{1,0:T(8,128)}) fusion(bf16[256,4096]{1,0:T(8,128)(2,1)} %all-gather.5.cloned.1.call-done, s32[256]{0:T(256)S(1)} %bitcast.43), kind=kOutput, calls=%fused_computation.34 | convolution fusion | flops 539033344 | bytes 6293504 | tf_op jit(solution)/shard_map/while/body/eval_jaxpr/dot_general | solution.py:41
  88.0 0.8 reshape.182
  88.8 1.2 slice_reduce_fusion
  90.0 0.8 reshape.168
  90.8 0.1 reshape.169
  90.9 0.3 copy.24
  91.2 5.0 %fusion.18 = f32[256,16]{0,1:T(8,128)S(1)} fusion(bf16[4096,16]{1,0:T(8,128)(2,1)S(1)} %reshape.168, f32[256,4096]{1,0:T(8,128)} %get-tuple-element.34, f32[256]{0:T(256)S(1)} %add_rsqrt_fusion), kind=kOutput, calls=%fused_computation.39 | convolution fusion | flops 202375168 | bytes 4342784 | tf_op jit(solution)/shard_map/while/body/eval_jaxpr/jvp()/dot_general | solution.py:14
  96.3 0.0 copy-done.2
  96.3 4.3 %multiply_reduce_fusion.1 = (f32[256]{0:T(256)S(1)}, f32[256,4096]{1,0:T(8,128)}) fusion(f32[256,4096]{1,0:T(8,128)S(1)} %copy-done.2, f32[256,16]{0,1:T(8,128)S(1)} %fusion.18, bf16[16,4096]{1,0:T(8,128)(2,1)S(1)} %reshape.169), kind=kOutput, calls=%fused_computation.33 | convolution fusion | flops 205520640 | bytes 8537088 | tf_op jit(solution)/shard_map/while/body/eval_jaxpr/jvp()/dot_general | solution.py:15
  100.6 7.2 %all-gather.7.cloned.1.call-done = bf16[256,4096]{1,0:T(8,128)(2,1)} async-done(((bf16[256,1024]{1,0:T(8,128)(2,1)}), bf16[256,4096]{1,0:T(8,128)(2,1)}) %all-gather.7.cloned.1.call-update) | async-done | bytes 2097168 | tf_op jit(solution)/shard_map/all_gather | solution.py:63
  107.8 3.9 %fusion.78 = (f32[256]{0:T(256)S(1)}, f32[256,256]{0,1:T(8,128)S(1)}) fusion(bf16[256,4096]{1,0:T(8,128)(2,1)} %all-gather.7.cloned.1.call-done, f32[256,4096]{1,0:T(8,128)} %get-tuple-element.36, f32[256]{0:T(256)S(1)} %fusion.60), kind=kOutput, calls=%fused_computation.118 | convolution fusion | flops 539098880 | bytes 6555648 | tf_op jit(solution)/shard_map/while/body/eval_jaxpr/jvp()/dot_general | solution.py:21
  111.7 0.1 select_reduce_fusion
  111.8 0.6 subtract_reduce_fusion
  112.4 0.1 copy-done.5
  112.5 0.9 fusion.10
  113.5 2.8 %fusion.76 = f32[256,16]{0,1:T(8,128)S(1)} fusion(bf16[16,4096]{1,0:T(8,128)(2,1)S(1)} %reshape.169, bf16[256,4096]{1,0:T(8,128)(2,1)S(1)} %get-tuple-element.40, f32[256,4096]{1,0:T(8,128)S(1)} %copy-done.4, f32[256]{0:T(256)S(1)} %multiply_multiply_fusion.1, f32[256]{0:T(256)S(1)} %fusion.60), kind=kOutput, calls=%fused_computation.117 | convolution fusion | flops 207618048 | bytes 6440960 | tf_op jit(solution)/shard_map/while/body/eval_jaxpr/transpose(jvp())/dot_general | solution.py:15
  116.3 0.0 copy-start.3
  116.3 3.1 %fusion.6 = f32[16,4096]{1,0:T(8,128)S(1)} fusion(f32[256,16]{0,1:T(8,128)S(1)} %fusion.18, bf16[16,4096]{1,0:T(8,128)(2,1)S(1)} %reshape.169, bf16[256,4096]{1,0:T(8,128)(2,1)S(1)} %get-tuple-element.40, f32[256,4096]{1,0:T(8,128)S(1)} %copy-done.4, f32[256]{0:T(256)S(1)} %multiply_multiply_fusion.1, f32[256]{0:T(256)S(1)} %fusion.60), kind=kOutput, calls=%fused_computation.21 | convolution fusion | flops 207814656 | bytes 6703104 | tf_op jit(solution)/shard_map/while/body/eval_jaxpr/transpose(jvp())/dot_general | solution.py:15
  119.4 2.5 fusion.7
  121.9 3.4 %fusion.15 = f32[256,16]{0,1:T(8,128)S(1)} fusion(f32[4096,16]{0,1:T(8,128)S(1)} %fusion.7, f32[256,4096]{1,0:T(8,128)S(1)} %copy-done.3, f32[256]{0:T(256)S(1)} %add_rsqrt_fusion), kind=kOutput, calls=%fused_computation.36 | convolution fusion | flops 202375168 | bytes 4473856 | tf_op jit(solution)/shard_map/while/body/eval_jaxpr/jvp()/dot_general | solution.py:14
  125.4 4.1 %multiply_reduce_fusion = (f32[256]{0:T(256)S(1)}, f32[256,4096]{1,0:T(8,128)S(1)}) fusion(f32[256,4096]{1,0:T(8,128)S(1)} %copy-done.3, f32[256,16]{0,1:T(8,128)S(1)} %fusion.15, f32[16,4096]{1,0:T(8,128)S(1)} %fusion.6), kind=kOutput, calls=%fused_computation.31 | convolution fusion | flops 205520640 | bytes 8668160 | tf_op jit(solution)/shard_map/while/body/eval_jaxpr/jvp()/dot_general | solution.py:15
  129.5 0.9 fusion.79
  130.4 0.1 fusion.41
  130.4 0.9 fusion.11
  131.4 4.2 %fusion.73 = f32[256,16]{0,1:T(8,128)S(1)} fusion(f32[16,4096]{1,0:T(8,128)S(1)} %fusion.6, bf16[256,4096]{1,0:T(8,128)(2,1)S(1)} %get-tuple-element.46, f32[256,4096]{1,0:T(8,128)S(1)} %get-tuple-element.42, f32[256]{0:T(256)S(1)} %multiply_multiply_fusion, f32[256]{0:T(256)S(1)} %fusion.61), kind=kOutput, calls=%fused_computation.116 | convolution fusion | flops 207618048 | bytes 6572032 | tf_op jit(solution)/shard_map/while/body/eval_jaxpr/transpose(jvp())/dot_general | solution.py:15
  135.6 2.9 %fusion.9 = bf16[16,4096]{1,0:T(8,128)(2,1)S(1)} fusion(f32[16,4096]{1,0:T(8,128)S(1)} %fusion.6, f32[256,16]{0,1:T(8,128)S(1)} %fusion.15, bf16[16,4096]{1,0:T(8,128)(2,1)S(1)} %reshape.169, bf16[256,4096]{1,0:T(8,128)(2,1)S(1)} %get-tuple-element.46, f32[256,4096]{1,0:T(8,128)S(1)} %get-tuple-element.42, f32[256]{0:T(256)S(1)} %multiply_multiply_fusion, ...), kind=kOutput, calls=%fused_computation.25 | convolution fusion | flops 207945728 | bytes 6834176 | tf_op jit(solution)/shard_map/while/body/eval_jaxpr/transpose(jvp())/dot_general | solution.py:15
  138.5 2.5 fusion.8
  141.0 0.5 copy.25
  141.5 1.2 concatenate.17
  142.7 0.2 concatenate.18
  142.9 0.1 pad_maximum_fusion
  143.0 0.4 copy.29
  143.4 2.2 reduce.5
  145.7 0.2 reshape.183
  145.8 14.9 %all_to_all.26 = bf16[8,2,8192]{2,1,0:T(2,128)(2,1)S(1)} all-to-all(bf16[8,2,8192]{2,1,0:T(2,128)(2,1)S(1)} %reshape.183), channel_id=1, replica_groups=mesh['head'=8,'client'=4] {'head'}, dimensions={0} | all-to-all | bytes 524288 | tf_op jit(solution)/shard_map/all_to_all | solution.py:84
  160.7 0.3 reshape.184
  161.0 1.0 copy.27
  162.0 0.0 all-reduce.2.cloned.1.call-start
  162.6 14.3 %all-gather.9.cloned.1.call-done = bf16[1,32,16384]{2,1,0:T(8,128)(2,1)} async-done(((bf16[1,8,16384]{2,1,0:T(8,128)(2,1)}), bf16[1,32,16384]{2,1,0:T(8,128)(2,1)}) %all-gather.9.cloned.1.call-update) | async-done | bytes 1048592 | tf_op jit(solution)/shard_map/all_gather | solution.py:85
  177.0 16.1 %fusion.30 = f32[32,1024]{1,0:T(8,128)} fusion(bf16[1024,16384]{1,0:T(8,128)(2,1)} %param.13, bf16[1,32,16384]{2,1,0:T(8,128)(2,1)} %all-gather.9.cloned.1.call-done), kind=kOutput, calls=%fused_computation.52 | convolution fusion | flops 1073741824 | bytes 34734080 | tf_op jit(solution)/shard_map/dot_general | solution.py:90
  193.0 0.0 all-reduce.2.cloned.1.call-update
  193.1 14.9 %convolution_convert_fusion = bf16[1024,16384]{1,0:T(8,128)(2,1)} fusion(bf16[1,32,16384]{2,1,0:T(8,128)(2,1)S(1)} %copy-done.6, f32[32,1024]{1,0:T(8,128)S(1)} %convolution_add_fusion), kind=kOutput, calls=%fused_computation.1 | convolution fusion | flops 1090584576 | bytes 34734080 | tf_op jit(solution)/shard_map/dot_general | solution.py:87
  207.9 55.7 %all-reduce.2.cloned.1.call-done = f32[32,1024]{1,0:T(8,128)} async-done(((f32[32,1024]{1,0:T(8,128)}), f32[32,1024]{1,0:T(8,128)}) %all-reduce.2.cloned.1.call-update) | async-done | bytes 131088 | tf_op jit(solution)/shard_map/psum | solution.py:95
  263.7 2.5 fusion.42
  (27 shorter events, 0.1 us)
Async XLA Ops:
  7.2 2.5 copy-start
  7.2 52.3 %reduce-scatter.2.cloned.1.call-start = ((), (), s32[]{:S(2)}) async-start(), calls=%async_computation.3 | async-start | bytes 2621440 | tf_op jit(solution)/shard_map/reduce_scatter | solution.py:70
  25.4 58.2 %copy-start.7 = (s32[1,256]{1,0:T(1,128)S(1)}, s32[1,256]{1,0:T(1,128)}, u32[]{:S(2)}) copy-start(s32[1,256]{1,0:T(1,128)} %param.14) | copy-start | bytes 3076
  25.4 58.2 %all-gather.5.cloned.1.call-start = ((), (), s32[]{:S(2)}) async-start(), calls=%async_computation.4 | async-start | bytes 2621440 | tf_op jit(solution)/shard_map/all_gather | solution.py:62
  26.2 81.6 %all-gather.7.cloned.1.call-start = ((), (), s32[]{:S(2)}) async-start(), calls=%async_computation.5 | async-start | bytes 2621440 | tf_op jit(solution)/shard_map/all_gather | solution.py:63
  62.8 25.2 %all-to-all-start = ((bf16[8,2,8192]{2,1,0:T(2,128)(2,1)}), bf16[8,2,8192]{2,1,0:T(2,128)(2,1)S(1)}, u32[]{:S(2)}, u32[]{:S(2)}) async-start(bf16[8,2,8192]{2,1,0:T(2,128)(2,1)} %reshape.181), calls=%async_computation.1 | async-start | bytes 524288 | tf_op jit(solution)/shard_map/all_to_all | solution.py:76
  68.3 108.7 %all-gather.9.cloned.1.call-start = ((), (), s32[]{:S(2)}) async-start(), calls=%async_computation.7 | async-start | bytes 1310720 | tf_op jit(solution)/shard_map/all_gather | solution.py:85
  91.2 5.1 %copy-start.2 = (f32[256,4096]{1,0:T(8,128)S(1)}, f32[256,4096]{1,0:T(8,128)}, u32[]{:S(2)}) copy-start(f32[256,4096]{1,0:T(8,128)} %get-tuple-element.34) | copy-start | bytes 12582916
  100.6 11.1 %copy-start.8 = (s32[1,256]{1,0:T(1,128)S(1)}, s32[1,256]{1,0:T(1,128)}, u32[]{:S(2)}) copy-start(s32[1,256]{1,0:T(1,128)} %param.15) | copy-start | bytes 3076
  107.8 4.6 %copy-start.4 = (f32[256,4096]{1,0:T(8,128)S(1)}, f32[256,4096]{1,0:T(8,128)}, u32[]{:S(2)}) copy-start(f32[256,4096]{1,0:T(8,128)} %get-tuple-element.36) | copy-start | bytes 12582916
  107.8 4.7 %copy-start.5 = (bf16[256,4096]{1,0:T(8,128)(2,1)S(1)}, bf16[256,4096]{1,0:T(8,128)(2,1)}, u32[]{:S(2)}) copy-start(bf16[256,4096]{1,0:T(8,128)(2,1)} %all-gather.7.cloned.1.call-done) | copy-start | bytes 6291460
  116.3 3.1 %copy-start.3 = (f32[256,4096]{1,0:T(8,128)S(1)}, f32[256,4096]{1,0:T(8,128)}, u32[]{:S(2)}) copy-start(f32[256,4096]{1,0:T(8,128)} %get-tuple-element.34) | copy-start | bytes 12582916
  162.0 101.7 %all-reduce.2.cloned.1.call-start = ((), (), s32[]{:S(2)}) async-start(), calls=%async_computation.6 | async-start | bytes 262144 | tf_op jit(solution)/shard_map/psum | solution.py:95
  177.0 16.1 %copy-start.6 = (bf16[1,32,16384]{2,1,0:T(8,128)(2,1)S(1)}, bf16[1,32,16384]{2,1,0:T(8,128)(2,1)}, u32[]{:S(2)}) copy-start(bf16[1,32,16384]{2,1,0:T(8,128)(2,1)} %all-gather.9.cloned.1.call-done) | copy-start | bytes 3145732
  193.1 73.1 %copy-start.1 = (bf16[256,1024]{1,0:T(8,128)(2,1)S(1)}, bf16[256,1024]{1,0:T(8,128)(2,1)}, u32[]{:S(2)}) copy-start(bf16[256,1024]{1,0:T(8,128)(2,1)} %param.11) | copy-start | bytes 1572868
Sparse Core Ops, SparseCore 0:
  25.6 33.9 reduce-scatter.1
  61.1 22.5 all-gather.4
  85.2 22.5 all-gather.6
  162.1 14.7 all-gather.8
  193.2 70.4 all-reduce.1
where the time goes:
time: 278 us; the launch traced here: 274 us
  waiting for transfers between devices  127 us (46%)
  matrix products  95 us (34%)
  between operations  15.9 us (6%)
  blocking collectives  14.9 us (5%)
  local copies, waits for them, and re-layouts  10.8 us (4%)
  starting transfers between devices  5.69 us (2%)
  other arithmetic  5.08 us (2%)
    psum x1, waiting for transfers between devices, local(): hidden_back = lax.psum(hidden_back, 'head')  55.7 us
    reduce_scatter x1, waiting for transfers between devices, local(): lax.psum_scatter(jnp.dot(hidden_rows, head_weight, preferred_element_type...  32.6 us
    dot_general x6, matrix products, client_loss(): jnp.dot(low_rank, factor_b, precision=lax.Precision.HIGHEST)  21.5 us
    dot_general x1, matrix products, local(): lax.dot_general(received, head_weight, (((1,), (1,)), ((), ())), preferre...  16.1 us
    all_gather x1, waiting for transfers between devices, local(): lax.all_gather(byte_table, 'client', axis=1, tiled=True)  15.3 us
    all_to_all x1, blocking collectives, local(): lax.all_to_all(deltas, 'head', split_axis=1, concat_axis=0, tiled=True)  14.9 us
    dot_general x1, matrix products, local(): lax.dot_general(hidden_rows, received, (((0,), (0,)), ((), ())), preferre...  14.9 us
    dot_general x1, matrix products, local(): jnp.dot(hidden_rows, head_weight, preferred_element_type=jnp.float32)  14.9 us
  transfers between devices with their start and end apart: 6, of which 5 were waited for; matrix products, arithmetic and copies ran while one was open for 13% of the time, Pallas kernels for 0%

commit v1 on v0

--- a/solution.py
+++ b/solution.py
@@ -5,6 +5,18 @@
 
 EPSILON = 1e-06
 learn_rate = 0.1
+
+
+def cut_along(array, dim, peers):
+    shape = array.shape
+    tiles = array.reshape(*shape[:dim], peers, shape[dim] // peers, *shape[dim + 1 :])
+    return jnp.moveaxis(tiles, dim, 0)
+
+
+def joined_along(blocks, dim):
+    blocks = jnp.moveaxis(blocks, 0, dim)
+    shape = blocks.shape
+    return blocks.reshape(*shape[:dim], shape[dim] * shape[dim + 1], *shape[dim + 2 :])
 
 
 def client_loss(factor_a, factor_b, inputs, label_row, out_table):
@@ -81,7 +93,14 @@
         return train_client(record[0], record[1], record[2], byte_full, out_full)
 
     deltas, losses = lax.map(run_client, (owned, tokens, labels))
-    returned = lax.all_to_all(deltas, "head", split_axis=1, concat_axis=0, tiled=True)
+    size, place = (lax.axis_size("head"), lax.axis_index("head"))
+    blocks = cut_along(deltas, 1, size)
+    outs = [blocks[place]]
+    for turn in range(1, size):
+        sent = blocks[(place + turn) % size]
+        outs.append(lax.ppermute(sent, "head", [(i, (i + turn) % size) for i in range(size)]))
+    blocks = jnp.stack(outs)[(place - jnp.arange(size)) % size]
+    returned = joined_along(blocks, 0)
     received = lax.all_gather(returned, "client", axis=0, tiled=True)
     hidden_rows = hidden
     grad_sum = lax.dot_general(

time: 278 us -> 281 us (1.011)
  blocking collectives: 14.9 us -> 0 us
  starting transfers between devices: 5.69 us -> 17.2 us
  waiting for transfers between devices: 127 us -> 131 us
    all_to_all x1 -> x0, blocking collectives: 14.9 us -> none  [local(): lax.all_to_all(deltas, 'head', split_axis=1, concat_axis=0, tiled=True)]
    ppermute x0 -> x7, starting transfers between devices: none -> 11.5 us  [local(): lax.ppermute(sent, 'head', [(i, (i + turn) % size) for i in range(size)])]
    ppermute x0 -> x7, waiting for transfers between devices: none -> 4.89 us  [local(): lax.ppermute(sent, 'head', [(i, (i + turn) % size) for i in range(size)])]
    squeeze x0 -> x2, other arithmetic: none -> 3.25 us  [local(): sent = blocks[(place + turn) % size]]
  transfers between devices with their start and end apart: 6 -> 13, of which waited for: 5 -> 8; matrix products, arithmetic and copies ran while one was open for 13% -> 14% of each run, Pallas kernels for 0% -> 0%
where the time goes in v1:
time: 281 us; the launch traced here: 277 us
  waiting for transfers between devices  131 us (47%)
  matrix products  95 us (34%)
  starting transfers between devices  17.2 us (6%)
  between operations  16.1 us (6%)
  local copies, waits for them, and re-layouts  11.2 us (4%)
  other arithmetic  6.01 us (2%)
    psum x1, waiting for transfers between devices, local(): hidden_back = lax.psum(hidden_back, 'head')  55.7 us
    reduce_scatter x1, waiting for transfers between devices, local(): lax.psum_scatter(jnp.dot(hidden_rows, head_weight, preferred_element_type...  32.4 us
    dot_general x6, matrix products, client_loss(): jnp.dot(low_rank, factor_b, precision=lax.Precision.HIGHEST)  21.5 us
    dot_general x1, matrix products, local(): lax.dot_general(received, head_weight, (((1,), (1,)), ((), ())), preferre...  16.1 us
    all_gather x1, waiting for transfers between devices, local(): lax.all_gather(byte_table, 'client', axis=1, tiled=True)  15.3 us
    dot_general x1, matrix products, local(): lax.dot_general(hidden_rows, received, (((0,), (0,)), ((), ())), preferre...  14.9 us
    dot_general x1, matrix products, local(): jnp.dot(hidden_rows, head_weight, preferred_element_type=jnp.float32)  14.9 us
    all_gather x1, waiting for transfers between devices, local(): received = lax.all_gather(returned, 'client', axis=0, tiled=True)  14 us
  transfers between devices with their start and end apart: 13, of which 8 were waited for; matrix products, arithmetic and copies ran while one was open for 14% of the time, Pallas kernels for 0%

profile of v1, /device:TPU:0, one launch (start us, length us, event | category | flops | bytes accessed | tf_op | source)
XLA Modules:
  0.0 276.6 jit_solution(5604636575862291413)
XLA Ops:
  7.2 0.8 reshape.209
  8.0 0.1 copy.21
  8.1 0.1 reshape.210
  8.2 1.5 gather_fusion
  9.7 0.9 convolution_add_fusion
  10.5 14.9 %fusion.71 = f32[32,16384]{1,0:T(8,128)} fusion(bf16[1024,16384]{1,0:T(8,128)(2,1)} %param.13, f32[32,1024]{1,0:T(8,128)S(1)} %convolution_add_fusion), kind=kOutput, calls=%fused_computation.119 | convolution fusion | flops 1073807360 | bytes 35782656 | tf_op jit(solution)/shard_map/dot_general | solution.py:83
  25.4 0.0 all-gather.5.cloned.1.call-start
  25.5 0.7 all-gather.5.cloned.1.call-update
  26.2 0.0 all-gather.7.cloned.1.call-start
  26.2 0.7 all-gather.7.cloned.1.call-update
  27.1 32.4 %reduce-scatter.2.cloned.1.call-done = f32[8,16384]{1,0:T(8,128)} async-done(((f32[32,16384]{1,0:T(8,128)}), f32[8,16384]{1,0:T(8,128)}) %reduce-scatter.2.cloned.1.call-update) | async-done | bytes 524304 | tf_op jit(solution)/shard_map/reduce_scatter | solution.py:82
  59.5 1.1 convert_bitcast_fusion
  60.6 0.5 broadcast.293
  61.1 0.8 reduce.4
  61.9 0.9 reshape.235
  62.8 5.5 %all-to-all-start = ((bf16[8,2,8192]{2,1,0:T(2,128)(2,1)}), bf16[8,2,8192]{2,1,0:T(2,128)(2,1)S(1)}, u32[]{:S(2)}, u32[]{:S(2)}) async-start(bf16[8,2,8192]{2,1,0:T(2,128)(2,1)} %reshape.235), calls=%async_computation.1 | async-start | bytes 524288 | tf_op jit(solution)/shard_map/all_to_all | solution.py:88
  68.3 15.3 %all-gather.5.cloned.1.call-done = bf16[256,4096]{1,0:T(8,128)(2,1)} async-done(((bf16[256,1024]{1,0:T(8,128)(2,1)}), bf16[256,4096]{1,0:T(8,128)(2,1)}) %all-gather.5.cloned.1.call-update) | async-done | bytes 2097168 | tf_op jit(solution)/shard_map/all_gather | solution.py:74
  83.7 4.4 %multiply_reduce_fusion.2 = (f32[256]{0:T(256)S(1)}, f32[256,4096]{1,0:T(8,128)}) fusion(bf16[256,4096]{1,0:T(8,128)(2,1)} %all-gather.5.cloned.1.call-done, s32[256]{0:T(256)S(1)} %bitcast.66), kind=kOutput, calls=%fused_computation.35 | convolution fusion | flops 539033344 | bytes 6293504 | tf_op jit(solution)/shard_map/while/body/eval_jaxpr/dot_general | solution.py:53
  88.0 0.8 reshape.236
  88.8 1.2 slice_reduce_fusion.1
  90.0 0.8 reshape.211
  90.8 0.1 reshape.212
  90.9 0.3 copy.23
  91.2 5.0 %fusion.18 = f32[256,16]{0,1:T(8,128)S(1)} fusion(bf16[4096,16]{1,0:T(8,128)(2,1)S(1)} %reshape.211, f32[256,4096]{1,0:T(8,128)} %get-tuple-element.42, f32[256]{0:T(256)S(1)} %add_rsqrt_fusion), kind=kOutput, calls=%fused_computation.40 | convolution fusion | flops 202375168 | bytes 4342784 | tf_op jit(solution)/shard_map/while/body/eval_jaxpr/jvp()/dot_general | solution.py:26
  96.3 4.3 %multiply_reduce_fusion.1 = (f32[256]{0:T(256)S(1)}, f32[256,4096]{1,0:T(8,128)}) fusion(f32[256,4096]{1,0:T(8,128)S(1)} %copy-done.2, f32[256,16]{0,1:T(8,128)S(1)} %fusion.18, bf16[16,4096]{1,0:T(8,128)(2,1)S(1)} %reshape.212), kind=kOutput, calls=%fused_computation.34 | convolution fusion | flops 205520640 | bytes 8537088 | tf_op jit(solution)/shard_map/while/body/eval_jaxpr/jvp()/dot_general | solution.py:27
  100.6 7.2 %all-gather.7.cloned.1.call-done = bf16[256,4096]{1,0:T(8,128)(2,1)} async-done(((bf16[256,1024]{1,0:T(8,128)(2,1)}), bf16[256,4096]{1,0:T(8,128)(2,1)}) %all-gather.7.cloned.1.call-update) | async-done | bytes 2097168 | tf_op jit(solution)/shard_map/all_gather | solution.py:75
  107.8 3.9 %fusion.92 = (f32[256]{0:T(256)S(1)}, f32[256,256]{0,1:T(8,128)S(1)}) fusion(bf16[256,4096]{1,0:T(8,128)(2,1)} %all-gather.7.cloned.1.call-done, f32[256,4096]{1,0:T(8,128)} %get-tuple-element.44, f32[256]{0:T(256)S(1)} %fusion.72), kind=kOutput, calls=%fused_computation.153 | convolution fusion | flops 539098880 | bytes 6555648 | tf_op jit(solution)/shard_map/while/body/eval_jaxpr/jvp()/dot_general | solution.py:33
  111.7 0.1 select_reduce_fusion
  111.8 0.6 subtract_reduce_fusion
  112.4 0.1 copy-done.5
  112.5 0.9 fusion.10
  113.5 2.8 %fusion.90 = f32[256,16]{0,1:T(8,128)S(1)} fusion(bf16[16,4096]{1,0:T(8,128)(2,1)S(1)} %reshape.212, bf16[256,4096]{1,0:T(8,128)(2,1)S(1)} %get-tuple-element.48, f32[256,4096]{1,0:T(8,128)S(1)} %copy-done.4, f32[256]{0:T(256)S(1)} %multiply_multiply_fusion.1, f32[256]{0:T(256)S(1)} %fusion.72), kind=kOutput, calls=%fused_computation.152 | convolution fusion | flops 207618048 | bytes 6440960 | tf_op jit(solution)/shard_map/while/body/eval_jaxpr/transpose(jvp())/dot_general | solution.py:27
  116.3 3.1 %fusion.6 = f32[16,4096]{1,0:T(8,128)S(1)} fusion(f32[256,16]{0,1:T(8,128)S(1)} %fusion.18, bf16[16,4096]{1,0:T(8,128)(2,1)S(1)} %reshape.212, bf16[256,4096]{1,0:T(8,128)(2,1)S(1)} %get-tuple-element.48, f32[256,4096]{1,0:T(8,128)S(1)} %copy-done.4, f32[256]{0:T(256)S(1)} %multiply_multiply_fusion.1, f32[256]{0:T(256)S(1)} %fusion.72), kind=kOutput, calls=%fused_computation.22 | convolution fusion | flops 207814656 | bytes 6703104 | tf_op jit(solution)/shard_map/while/body/eval_jaxpr/transpose(jvp())/dot_general | solution.py:27
  119.4 2.5 fusion.7
  121.9 3.4 %fusion.15 = f32[256,16]{0,1:T(8,128)S(1)} fusion(f32[4096,16]{0,1:T(8,128)S(1)} %fusion.7, f32[256,4096]{1,0:T(8,128)S(1)} %copy-done.3, f32[256]{0:T(256)S(1)} %add_rsqrt_fusion), kind=kOutput, calls=%fused_computation.37 | convolution fusion | flops 202375168 | bytes 4473856 | tf_op jit(solution)/shard_map/while/body/eval_jaxpr/jvp()/dot_general | solution.py:26
  125.4 4.1 %multiply_reduce_fusion = (f32[256]{0:T(256)S(1)}, f32[256,4096]{1,0:T(8,128)S(1)}) fusion(f32[256,4096]{1,0:T(8,128)S(1)} %copy-done.3, f32[256,16]{0,1:T(8,128)S(1)} %fusion.15, f32[16,4096]{1,0:T(8,128)S(1)} %fusion.6), kind=kOutput, calls=%fused_computation.32 | convolution fusion | flops 205520640 | bytes 8668160 | tf_op jit(solution)/shard_map/while/body/eval_jaxpr/jvp()/dot_general | solution.py:27
  129.5 0.9 fusion.93
  130.4 0.1 fusion.38
  130.4 0.9 fusion.11
  131.4 4.2 %fusion.87 = f32[256,16]{0,1:T(8,128)S(1)} fusion(f32[16,4096]{1,0:T(8,128)S(1)} %fusion.6, bf16[256,4096]{1,0:T(8,128)(2,1)S(1)} %get-tuple-element.54, f32[256,4096]{1,0:T(8,128)S(1)} %get-tuple-element.50, f32[256]{0:T(256)S(1)} %multiply_multiply_fusion, f32[256]{0:T(256)S(1)} %fusion.73), kind=kOutput, calls=%fused_computation.151 | convolution fusion | flops 207618048 | bytes 6572032 | tf_op jit(solution)/shard_map/while/body/eval_jaxpr/transpose(jvp())/dot_general | solution.py:27
  135.6 2.9 %fusion.9 = bf16[16,4096]{1,0:T(8,128)(2,1)S(1)} fusion(f32[16,4096]{1,0:T(8,128)S(1)} %fusion.6, f32[256,16]{0,1:T(8,128)S(1)} %fusion.15, bf16[16,4096]{1,0:T(8,128)(2,1)S(1)} %reshape.212, bf16[256,4096]{1,0:T(8,128)(2,1)S(1)} %get-tuple-element.54, f32[256,4096]{1,0:T(8,128)S(1)} %get-tuple-element.50, f32[256]{0:T(256)S(1)} %multiply_multiply_fusion, ...), kind=kOutput, calls=%fused_computation.26 | convolution fusion | flops 207945728 | bytes 6834176 | tf_op jit(solution)/shard_map/while/body/eval_jaxpr/transpose(jvp())/dot_general | solution.py:27
  138.5 2.5 fusion.8
  141.0 0.5 copy.24
  141.5 1.2 concatenate.16
  142.7 0.2 concatenate.17
  142.9 0.5 fusion.64
  143.4 3.4 %collective-permute-start.4 = (bf16[1,16384]{1,0:T(2,128)(2,1)S(1)}, bf16[1,16384]{1,0:T(2,128)(2,1)S(1)}, u32[]{:S(2)}, u32[]{:S(2)}) collective-permute-start(bf16[1,16384]{1,0:T(2,128)(2,1)S(1)} %get-tuple-element.38), channel_id=1, source_target_pairs={{0,20},{4,24},{8,28},{12,0},{16,4},{20,8},{24,12},{28,16},{1,21},{... | collective-permute-start | bytes 98312 | tf_op jit(solution)/shard_map/ppermute | solution.py:101
  146.8 1.7 collective-permute-start.5
  148.4 2.8 fusion.70
  151.2 1.6 collective-permute-start.2
  152.8 0.1 collective-permute-start.3
  152.8 2.8 %collective-permute-start.6 = (bf16[1,16384]{1,0:T(2,128)(2,1)S(1)}, bf16[1,16384]{1,0:T(2,128)(2,1)S(1)}, u32[]{:S(2)}, u32[]{:S(2)}) collective-permute-start(bf16[1,16384]{1,0:T(2,128)(2,1)S(1)} %get-tuple-element.23), channel_id=1, source_target_pairs={{0,28},{4,0},{8,4},{12,8},{16,12},{20,16},{24,20},{28,24},{1,29},{... | collective-permute-start | bytes 98312 | tf_op jit(solution)/shard_map/ppermute | solution.py:101
  155.6 2.0 collective-permute-start.1
  157.7 2.0 collective-permute-done.2
  159.7 0.7 collective-permute-done.3
  160.3 2.2 collective-permute-done
  162.6 0.8 stack.31
  163.4 1.4 gather_fusion.1
  164.8 0.0 all-reduce.2.cloned.1.call-start
  165.5 14.0 %all-gather.9.cloned.1.call-done = bf16[32,16384]{1,0:T(8,128)(2,1)} async-done(((bf16[8,16384]{1,0:T(8,128)(2,1)}), bf16[32,16384]{1,0:T(8,128)(2,1)}) %all-gather.9.cloned.1.call-update) | async-done | bytes 1048592 | tf_op jit(solution)/shard_map/all_gather | solution.py:104
  179.5 16.1 %fusion.94 = f32[32,1024]{1,0:T(8,128)} fusion(bf16[32,16384]{1,0:T(8,128)(2,1)} %all-gather.9.cloned.1.call-done, bf16[1024,16384]{1,0:T(8,128)(2,1)} %param.13), kind=kOutput, calls=%fused_computation.155 | convolution fusion | flops 1073741824 | bytes 34734080 | tf_op jit(solution)/shard_map/dot_general | solution.py:109
  195.6 14.9 %convolution_convert_fusion = bf16[1024,16384]{1,0:T(8,128)(2,1)} fusion(bf16[32,16384]{1,0:T(8,128)(2,1)S(1)} %copy-done.6, f32[32,1024]{1,0:T(8,128)S(1)} %convolution_add_fusion), kind=kOutput, calls=%fused_computation.2 | convolution fusion | flops 1090584576 | bytes 34734080 | tf_op jit(solution)/shard_map/dot_general | solution.py:106
  210.5 55.7 %all-reduce.2.cloned.1.call-done = f32[32,1024]{1,0:T(8,128)} async-done(((f32[32,1024]{1,0:T(8,128)}), f32[32,1024]{1,0:T(8,128)}) %all-reduce.2.cloned.1.call-update) | async-done | bytes 131088 | tf_op jit(solution)/shard_map/psum | solution.py:114
  266.2 2.5 fusion.39
  (40 shorter events, 0.3 us)
Async XLA Ops:
  7.2 2.5 copy-start
  7.2 52.3 %reduce-scatter.2.cloned.1.call-start = ((), (), s32[]{:S(2)}) async-start(), calls=%async_computation.2 | async-start | bytes 2621440 | tf_op jit(solution)/shard_map/reduce_scatter | solution.py:82
  25.4 58.2 %copy-start.7 = (s32[1,256]{1,0:T(1,128)S(1)}, s32[1,256]{1,0:T(1,128)}, u32[]{:S(2)}) copy-start(s32[1,256]{1,0:T(1,128)} %param.14) | copy-start | bytes 3076
  25.4 58.2 %all-gather.5.cloned.1.call-start = ((), (), s32[]{:S(2)}) async-start(), calls=%async_computation.3 | async-start | bytes 2621440 | tf_op jit(solution)/shard_map/all_gather | solution.py:74
  26.2 81.6 %all-gather.7.cloned.1.call-start = ((), (), s32[]{:S(2)}) async-start(), calls=%async_computation.4 | async-start | bytes 2621440 | tf_op jit(solution)/shard_map/all_gather | solution.py:75
  62.8 25.2 %all-to-all-start = ((bf16[8,2,8192]{2,1,0:T(2,128)(2,1)}), bf16[8,2,8192]{2,1,0:T(2,128)(2,1)S(1)}, u32[]{:S(2)}, u32[]{:S(2)}) async-start(bf16[8,2,8192]{2,1,0:T(2,128)(2,1)} %reshape.235), calls=%async_computation.1 | async-start | bytes 524288 | tf_op jit(solution)/shard_map/all_to_all | solution.py:88
  68.3 111.2 %all-gather.9.cloned.1.call-start = ((), (), s32[]{:S(2)}) async-start(), calls=%async_computation.6 | async-start | bytes 1310720 | tf_op jit(solution)/shard_map/all_gather | solution.py:104
  91.2 5.1 %copy-start.2 = (f32[256,4096]{1,0:T(8,128)S(1)}, f32[256,4096]{1,0:T(8,128)}, u32[]{:S(2)}) copy-start(f32[256,4096]{1,0:T(8,128)} %get-tuple-element.42) | copy-start | bytes 12582916
  100.6 11.1 %copy-start.8 = (s32[1,256]{1,0:T(1,128)S(1)}, s32[1,256]{1,0:T(1,128)}, u32[]{:S(2)}) copy-start(s32[1,256]{1,0:T(1,128)} %param.15) | copy-start | bytes 3076
  107.8 4.6 %copy-start.4 = (f32[256,4096]{1,0:T(8,128)S(1)}, f32[256,4096]{1,0:T(8,128)}, u32[]{:S(2)}) copy-start(f32[256,4096]{1,0:T(8,128)} %get-tuple-element.44) | copy-start | bytes 12582916
  107.8 4.7 %copy-start.5 = (bf16[256,4096]{1,0:T(8,128)(2,1)S(1)}, bf16[256,4096]{1,0:T(8,128)(2,1)}, u32[]{:S(2)}) copy-start(bf16[256,4096]{1,0:T(8,128)(2,1)} %all-gather.7.cloned.1.call-done) | copy-start | bytes 6291460
  116.3 3.1 %copy-start.3 = (f32[256,4096]{1,0:T(8,128)S(1)}, f32[256,4096]{1,0:T(8,128)}, u32[]{:S(2)}) copy-start(f32[256,4096]{1,0:T(8,128)} %get-tuple-element.42) | copy-start | bytes 12582916
  143.4 12.2 %collective-permute-start.4 = (bf16[1,16384]{1,0:T(2,128)(2,1)S(1)}, bf16[1,16384]{1,0:T(2,128)(2,1)S(1)}, u32[]{:S(2)}, u32[]{:S(2)}) collective-permute-start(bf16[1,16384]{1,0:T(2,128)(2,1)S(1)} %get-tuple-element.38), channel_id=1, source_target_pairs={{0,20},{4,24},{8,28},{12,0},{16,4},{20,8},{24,12},{28,16},{1,21},{... | collective-permute-start | bytes 98312 | tf_op jit(solution)/shard_map/ppermute | solution.py:101
  146.8 8.9 %collective-permute-start.5 = (bf16[1,16384]{1,0:T(2,128)(2,1)S(1)}, bf16[1,16384]{1,0:T(2,128)(2,1)S(1)}, u32[]{:S(2)}, u32[]{:S(2)}) collective-permute-start(bf16[1,16384]{1,0:T(2,128)(2,1)S(1)} %get-tuple-element.37), channel_id=1, source_target_pairs={{0,24},{4,28},{8,0},{12,4},{16,8},{20,12},{24,16},{28,20},{1,25},{... | collective-permute-start | bytes 98312 | tf_op jit(solution)/shard_map/ppermute | solution.py:101
  151.2 8.5 %collective-permute-start.2 = (bf16[1,16384]{1,0:T(2,128)(2,1)S(1)}, bf16[1,16384]{1,0:T(2,128)(2,1)S(1)}, u32[]{:S(2)}, u32[]{:S(2)}) collective-permute-start(bf16[1,16384]{1,0:T(2,128)(2,1)S(1)} %get-tuple-element.35), channel_id=1, source_target_pairs={{0,12},{4,16},{8,20},{12,24},{16,28},{20,0},{24,4},{28,8},{1,13},{... | collective-permute-start | bytes 98312 | tf_op jit(solution)/shard_map/ppermute | solution.py:101
  152.8 7.6 %collective-permute-start.3 = (bf16[1,16384]{1,0:T(2,128)(2,1)S(1)}, bf16[1,16384]{1,0:T(2,128)(2,1)S(1)}, u32[]{:S(2)}, u32[]{:S(2)}) collective-permute-start(bf16[1,16384]{1,0:T(2,128)(2,1)S(1)} %get-tuple-element.36), channel_id=1, source_target_pairs={{0,16},{4,20},{8,24},{12,28},{16,0},{20,4},{24,8},{28,12},{1,17},{... | collective-permute-start | bytes 98312 | tf_op jit(solution)/shard_map/ppermute | solution.py:101
  152.8 7.5 %collective-permute-start.6 = (bf16[1,16384]{1,0:T(2,128)(2,1)S(1)}, bf16[1,16384]{1,0:T(2,128)(2,1)S(1)}, u32[]{:S(2)}, u32[]{:S(2)}) collective-permute-start(bf16[1,16384]{1,0:T(2,128)(2,1)S(1)} %get-tuple-element.23), channel_id=1, source_target_pairs={{0,28},{4,0},{8,4},{12,8},{16,12},{20,16},{24,20},{28,24},{1,29},{... | collective-permute-start | bytes 98312 | tf_op jit(solution)/shard_map/ppermute | solution.py:101
  155.6 7.0 %collective-permute-start = (bf16[1,16384]{1,0:T(2,128)(2,1)S(1)}, bf16[1,16384]{1,0:T(2,128)(2,1)S(1)}, u32[]{:S(2)}, u32[]{:S(2)}) collective-permute-start(bf16[1,16384]{1,0:T(2,128)(2,1)S(1)} %get-tuple-element.33), channel_id=1, source_target_pairs={{0,4},{4,8},{8,12},{12,16},{16,20},{20,24},{24,28},{28,0},{1,5},{5... | collective-permute-start | bytes 98312 | tf_op jit(solution)/shard_map/ppermute | solution.py:101
  155.6 6.9 %collective-permute-start.1 = (bf16[1,16384]{1,0:T(2,128)(2,1)S(1)}, bf16[1,16384]{1,0:T(2,128)(2,1)S(1)}, u32[]{:S(2)}, u32[]{:S(2)}) collective-permute-start(bf16[1,16384]{1,0:T(2,128)(2,1)S(1)} %get-tuple-element.34), channel_id=1, source_target_pairs={{0,8},{4,12},{8,16},{12,20},{16,24},{20,28},{24,0},{28,4},{1,9},{5... | collective-permute-start | bytes 98312 | tf_op jit(solution)/shard_map/ppermute | solution.py:101
  164.8 101.4 %all-reduce.2.cloned.1.call-start = ((), (), s32[]{:S(2)}) async-start(), calls=%async_computation.5 | async-start | bytes 262144 | tf_op jit(solution)/shard_map/psum | solution.py:114
  179.5 16.1 %copy-start.6 = (bf16[32,16384]{1,0:T(8,128)(2,1)S(1)}, bf16[32,16384]{1,0:T(8,128)(2,1)}, u32[]{:S(2)}) copy-start(bf16[32,16384]{1,0:T(8,128)(2,1)} %all-gather.9.cloned.1.call-done) | copy-start | bytes 3145732
  195.6 73.1 %copy-start.1 = (bf16[256,1024]{1,0:T(8,128)(2,1)S(1)}, bf16[256,1024]{1,0:T(8,128)(2,1)}, u32[]{:S(2)}) copy-start(bf16[256,1024]{1,0:T(8,128)(2,1)} %param.11) | copy-start | bytes 1572868
Sparse Core Ops, SparseCore 0:
  25.6 33.9 reduce-scatter.1
  61.1 22.5 all-gather.4
  85.2 22.5 all-gather.6
  165.0 14.5 all-gather.8
  195.7 70.4 all-reduce.1
